TPU v7x, 128 devices: a whole 4x4x4 slice. The times are simulated.
128 devices in a mesh: sph: 16 (over x_lo, z, core), rad: 8 (over y, x_hi).
Axes of the slice: x: 4 (x_hi: 2, x_lo: 2; x = x_hi * 2 + x_lo), y: 4, z: 4, core: 2. Of those that a mesh axis runs over, the one named last changes fastest.
Arguments:
- coeffs: bfloat16 [65536, 480], P('sph'), may hold values from -6 to 6
- interp: bfloat16 [65536, 2048], P('sph', 'rad'), may hold values from -0.055664062 to 0.055664062
- phases: float32 [64, 2048], P(None, 'rad'), may hold values from 0.3 to 3
- tables: bfloat16 [16, 480, 480], P('rad'), may hold values from -0.25 to 0.25
- bins: int32 [65536], P('sph'), may hold values from 0 to 63
Outputs:
- fields: bfloat16 [65536, 480], P('sph', 'rad')
All inputs are finite; a program needn't handle non-finite values.
Results may differ from a plain program's by a relative error of at most 0.024.
Values may be sent and summed in bfloat16 or wider, within the bound.
A program may use at most 64 MiB of HBM per device.

v0:
```python
import jax
import jax.numpy as jnp
from jax import lax
from jax.sharding import PartitionSpec as P


def in_blocks(shard, dim, size):
    lengths = shard.shape
    pieces = shard.reshape(*lengths[:dim], size, lengths[dim] // size, *lengths[dim + 1 :])
    return jnp.moveaxis(pieces, dim, 0)


def summed_on_arrival(shard, axis, dim):
    pieces = in_blocks(shard, dim, lax.axis_size(axis))
    arrived = lax.all_to_all(pieces, axis, split_axis=0, concat_axis=0, tiled=True)
    return arrived.astype(jnp.float32).sum(axis=0)


def from_everyone(shard, axis):
    copies = jnp.broadcast_to(shard, (lax.axis_size(axis), *shard.shape))
    return lax.all_to_all(copies, axis, split_axis=0, concat_axis=0, tiled=True)


def in_order(pieces, dim):
    pieces = jnp.moveaxis(pieces, 0, dim)
    lengths = pieces.shape
    return pieces.reshape(*lengths[:dim], lengths[dim] * lengths[dim + 1], *lengths[dim + 2 :])


def gather_directly(shard, axis, dim):
    pieces = from_everyone(shard, axis)
    return in_order(pieces, dim)


def body(coeffs, interp, phases, tables, bins):
    node_rows = interp.shape[1]
    onehot = (bins[:, None] == jnp.arange(phases.shape[0], dtype=jnp.int32)[None, :]).astype(
        jnp.float32
    )
    lifted = jnp.dot(onehot, phases, preferred_element_type=jnp.float32)
    proj = (interp.astype(jnp.float32) * lifted).astype(jnp.bfloat16)
    partial_nodes = jnp.einsum("sr,sc->rc", proj, coeffs, preferred_element_type=jnp.float32)
    share = summed_on_arrival(partial_nodes.astype(jnp.bfloat16), "sph", 0)
    rows = share.shape[0]
    first = lax.axis_index("sph") * rows
    which = first // (node_rows // tables.shape[0])
    table = lax.dynamic_index_in_dim(tables, which, 0, keepdims=False)
    local_part = jnp.dot(
        share.astype(jnp.bfloat16), table, preferred_element_type=jnp.float32
    ).astype(jnp.bfloat16)
    angular = gather_directly(local_part, "sph", 0)
    own_spheres = lax.all_to_all(proj, "rad", split_axis=0, concat_axis=1, tiled=True)
    all_angular = gather_directly(angular, "rad", 0)
    own_fields = jnp.dot(own_spheres, all_angular, preferred_element_type=jnp.float32).astype(
        jnp.bfloat16
    )
    fields = lax.all_to_all(own_fields, "rad", split_axis=1, concat_axis=0, tiled=True)
    return fields


def solution(mesh):
    return jax.shard_map(
        body,
        mesh=mesh,
        in_specs=(P("sph", None), P("sph", "rad"), P(None, "rad"), P("rad", None, None), P("sph")),
        out_specs=P("sph", "rad"),
        check_vma=False,
    )
```

profile of v0, /device:TPU:1, one launch (start us, length us, event | category | flops | bytes accessed | tf_op | source)
XLA Modules:
  0.0 115.1 jit_solution(1360990137777865106)
XLA Ops:
  0.0 0.0 copy-start
  0.0 0.0 copy-start.1
  0.0 3.5 %fusion = bf16[4096,256]{1,0:T(8,128)(2,1)} fusion(f32[64,256]{1,0:T(8,128)} %param.7, bf16[4096,256]{1,0:T(8,128)(2,1)} %param.6, s32[4096]{0:T(1024)} %param.9), kind=kOutput, calls=%fused_computation.1 | convolution fusion | flops 137625600 | bytes 4276224 | tf_op jit(solution)/shard_map/dot_general | solution.py:40
  3.5 0.0 copy-done.1
  3.5 2.8 %convolution_convert_fusion = bf16[256,480]{0,1:T(8,128)(2,1)S(1)} fusion(bf16[4096,480]{0,1:T(8,128)(2,1)S(1)} %copy-done.1, bf16[4096,256]{1,0:T(8,128)(2,1)} %fusion), kind=kOutput, calls=%fused_computation.7 | convolution fusion | flops 1006755840 | bytes 6275072 | tf_op jit(solution)/shard_map/sr,sc->rc/dot_general | solution.py:42
  6.3 0.8 copy.10
  7.2 7.7 %all-to-all-start.1 = ((bf16[16,16,480]{2,1,0:T(8,128)(2,1)}), bf16[16,16,480]{2,1,0:T(8,128)(2,1)S(1)}, u32[]{:S(2)}, u32[]{:S(2)}) async-start(bf16[16,16,480]{2,1,0:T(8,128)(2,1)} %bitcast.2), calls=%async_computation.1 | async-start | bytes 524288 | tf_op jit(solution)/shard_map/all_to_all | solution.py:15
  14.9 7.2 %all-to-all-done.1 = bf16[16,16,480]{2,1,0:T(8,128)(2,1)S(1)} async-done(((bf16[16,16,480]{2,1,0:T(8,128)(2,1)}), bf16[16,16,480]{2,1,0:T(8,128)(2,1)S(1)}, u32[]{:S(2)}, u32[]{:S(2)}) %all-to-all-start.1) | async-done | bytes 245792 | tf_op jit(solution)/shard_map/all_to_all | solution.py:15
  22.1 0.1 reduce_sum.12
  22.1 0.0 copy-done
  22.2 0.2 convolution_convert_fusion.1
  22.4 10.6 %all_to_all.50 = bf16[16,16,480]{2,1,0:T(8,128)(2,1)S(1)} all-to-all(bf16[16,16,480]{2,1,0:T(8,128)(2,1)S(1)} %broadcast_in_dim.8), channel_id=1, replica_groups=mesh['sph'=16,'rad'=8] {'sph'}, dimensions={0} | all-to-all | bytes 491520 | tf_op jit(solution)/shard_map/all_to_all | solution.py:21
  33.0 6.4 %all-to-all-start = ((bf16[8,512,256]{2,1,0:T(8,128)(2,1)}), bf16[8,512,256]{2,1,0:T(8,128)(2,1)S(1)}, u32[]{:S(2)}, u32[]{:S(2)}) async-start(bf16[8,512,256]{2,1,0:T(8,128)(2,1)} %bitcast), calls=%async_computation | async-start | bytes 4194304 | tf_op jit(solution)/shard_map/all_to_all | solution.py:52
  39.3 0.8 copy.11
  40.2 26.5 %all-to-all-done = bf16[8,512,256]{2,1,0:T(8,128)(2,1)S(1)} async-done(((bf16[8,512,256]{2,1,0:T(8,128)(2,1)}), bf16[8,512,256]{2,1,0:T(8,128)(2,1)S(1)}, u32[]{:S(2)}, u32[]{:S(2)}) %all-to-all-start) | async-done | bytes 2097184 | tf_op jit(solution)/shard_map/all_to_all | solution.py:52
  66.7 1.1 broadcast_in_dim.9
  67.7 30.1 %all_to_all.51 = bf16[8,256,480]{1,2,0:T(8,128)(2,1)S(1)} all-to-all(bf16[8,256,480]{1,2,0:T(8,128)(2,1)S(1)} %broadcast_in_dim.9), channel_id=1, replica_groups=mesh['sph'=16,'rad'=8] {'rad'}, dimensions={0} | all-to-all | bytes 3932160 | tf_op jit(solution)/shard_map/all_to_all | solution.py:21
  97.9 2.0 %fusion.6 = bf16[512,480]{0,1:T(8,128)(2,1)} fusion(bf16[8,256,480]{1,2,0:T(8,128)(2,1)S(1)} %all_to_all.51, bf16[8,512,256]{2,1,0:T(8,128)(2,1)S(1)} %all-to-all-done), kind=kOutput, calls=%fused_computation.6 | convolution fusion | flops 1006878720 | bytes 4554752 | tf_op jit(solution)/shard_map/dot_general | solution.py:54
  99.9 1.1 all_to_all.41
  101.0 12.8 %all_to_all.52 = bf16[512,8,60]{0,2,1:T(8,128)(2,1)S(1)} all-to-all(bf16[512,8,60]{0,2,1:T(8,128)(2,1)S(1)} %all_to_all.41), channel_id=1, replica_groups=mesh['sph'=16,'rad'=8] {'rad'}, dimensions={1} | all-to-all | bytes 983040 | tf_op jit(solution)/shard_map/all_to_all | solution.py:57
  113.8 0.3 copy.15
  114.1 1.0 copy.13
  (2 shorter events, 0.1 us)
Async XLA Ops:
  0.0 22.1 %copy-start = (bf16[2,480,480]{2,1,0:T(8,128)(2,1)S(1)}, bf16[2,480,480]{2,1,0:T(8,128)(2,1)}, u32[]{:S(2)}) copy-start(bf16[2,480,480]{2,1,0:T(8,128)(2,1)} %param.8) | copy-start | bytes 2764804
  0.0 3.5 %copy-start.1 = (bf16[4096,480]{0,1:T(8,128)(2,1)S(1)}, bf16[4096,480]{0,1:T(8,128)(2,1)}, u32[]{:S(2)}) copy-start(bf16[4096,480]{0,1:T(8,128)(2,1)} %param.5) | copy-start | bytes 11796484
  7.2 14.9 %all-to-all-start.1 = ((bf16[16,16,480]{2,1,0:T(8,128)(2,1)}), bf16[16,16,480]{2,1,0:T(8,128)(2,1)S(1)}, u32[]{:S(2)}, u32[]{:S(2)}) async-start(bf16[16,16,480]{2,1,0:T(8,128)(2,1)} %bitcast.2), calls=%async_computation.1 | async-start | bytes 524288 | tf_op jit(solution)/shard_map/all_to_all | solution.py:15
  33.0 33.7 %all-to-all-start = ((bf16[8,512,256]{2,1,0:T(8,128)(2,1)}), bf16[8,512,256]{2,1,0:T(8,128)(2,1)S(1)}, u32[]{:S(2)}, u32[]{:S(2)}) async-start(bf16[8,512,256]{2,1,0:T(8,128)(2,1)} %bitcast), calls=%async_computation | async-start | bytes 4194304 | tf_op jit(solution)/shard_map/all_to_all | solution.py:52
where the time goes:
time: 117 us; the launch traced here: 115 us
  blocking collectives  53.5 us (46%)
  waiting for transfers between devices  33.7 us (29%)
  starting transfers between devices  14.1 us (12%)
  matrix products  8.47 us (7%)
  local copies, waits for them, and re-layouts  5.19 us (4%)
    all_to_all x2, blocking collectives, from_everyone(): return lax.all_to_all(copies, axis, split_axis=0, concat_axis=0, tiled=True)  40.7 us
    all_to_all x1, waiting for transfers between devices, body(): lax.all_to_all(proj, 'rad', split_axis=0, concat_axis=1, tiled=True)  26.5 us
    all_to_all x1, blocking collectives, body(): lax.all_to_all(own_fields, 'rad', split_axis=1, concat_axis=0, tiled=True)  12.8 us
    all_to_all x1, starting transfers between devices, summed_on_arrival(): lax.all_to_all(pieces, axis, split_axis=0, concat_axis=0, tiled=True)  7.74 us
    all_to_all x1, waiting for transfers between devices, summed_on_arrival(): lax.all_to_all(pieces, axis, split_axis=0, concat_axis=0, tiled=True)  7.19 us
    all_to_all x1, starting transfers between devices, body(): lax.all_to_all(proj, 'rad', split_axis=0, concat_axis=1, tiled=True)  6.36 us
    dot_general x1, matrix products, body(): lifted = jnp.dot(onehot, phases, preferred_element_type=jnp.float32)  3.5 us
    dot_general x1, matrix products, body(): jnp.einsum('sr,sc->rc', proj, coeffs, preferred_element_type=jnp.float32)  2.8 us
  transfers between devices with their start and end apart: 2, of which 2 were waited for; matrix products, arithmetic and copies ran while one was open for 1% of the time, Pallas kernels for 0%

commit v1 on v0

v1 whole, which is shorter than its diff:
```python
import functools

import jax
import jax.numpy as jnp
from jax import lax
from jax.experimental import pallas as pl
from jax.experimental.pallas import tpu as pltpu
from jax.sharding import PartitionSpec as P

MESH = pl.DeviceIdType.MESH
BF = jnp.bfloat16
F32 = jnp.float32

OFF = [(2, 1), (2, 0), (1, 1), (1, 0), (3, 1), (3, 0), (0, 1), (0, 0)]
XK = [k for k, (dy, dx) in enumerate(OFF) if dx]
NQ = [4 if dx else 2 for dy, dx in OFF[:7]]
BASE = [sum(NQ[:k]) for k in range(7)]
NPIECE = sum(NQ)
FIRST = {0: 2, 1: 2, 2: 2, 3: 2, 4: 1, 5: 2, 6: 1}
SECOND = [(4, 1), (6, 1)]
THIRD = [(k, q) for q in (2, 3) for k in XK]


def where():
    s, r = lax.axis_index("sph"), lax.axis_index("rad")
    return (r % 2) * 2 + s // 8, r // 2, (s // 2) % 4, s % 2


def device(x, y, z, c):
    x, y, z, c = x % 4, y % 4, z % 4, c % 2
    return (x % 2) * 8 + z * 2 + c, y * 2 + x // 2


def kernel(
    coeffs, interp, phases, tables, bins, out,
    interp_v, coeffs_v, phases_v, bins_v, table_v, phl_v, perm_v, proj_v, recv_v, acc_v, part_v,
    rs_v, xs_v, xr_v, ang_v, fsend_v, frecv_v, out_v,
    in_sem, co_sem, small_sem, ps_sem, pr_sem, rss_sem, rsr_sem, xx_sem, pls_sem, plr_sem,
    zs_sem, zr_sem, cs_sem, cr_sem, fs_sem, fr_sem, out_sem,
):
    x, y, z, c = where()
    xh, xl = x // 2, x % 2
    rad, slot = y * 2 + xh, z * 2 + c
    rows = pl.multiple_of(slot * 32, 32)

    def chunk_of(k):
        dy, dx = OFF[k]
        return ((y + dy) % 4) * 2 + (xh + dx) % 2

    loads = [
        pltpu.make_async_copy(phases, phases_v, small_sem.at[0]),
        pltpu.make_async_copy(bins, bins_v, small_sem.at[1]),
    ]
    inters, coefs = [], []
    for k in range(8):
        at = pl.ds(pl.multiple_of(chunk_of(k) * 512, 512), 512)
        inters.append(pltpu.make_async_copy(interp.at[at, :], interp_v.at[k], in_sem.at[k]))
        coefs.append(pltpu.make_async_copy(coeffs.at[at, :], coeffs_v.at[k], co_sem.at[k]))
    table = pltpu.make_async_copy(tables.at[slot // 4], table_v, small_sem.at[2])
    for load in [*loads, *inters, *coefs, table]:
        load.start()

    partners = [(x + 2 * dx, y + dy, z, c) for dy, dx in OFF[:7]]
    partners += [(x, y, z + dz, c + dc) for dz in range(4) for dc in range(2) if dz or dc]
    partners += [(x + 1 - 2 * xl, y, z, c)]
    partners += [(3 - x, y + dy, z, c) for dy in range(4)]
    barrier = pltpu.get_barrier_semaphore()
    for partner in partners:
        pl.semaphore_signal(barrier, inc=1, device_id=device(*partner), device_id_type=MESH)

    for load in loads:
        load.wait()
    ph = phases_v[...]
    hi = ph.astype(BF)
    phl_v[0:64, :] = hi
    phl_v[64:128, :] = (ph - hi.astype(F32)).astype(BF)

    def send(src, dst, ssem, rsem, to):
        return pltpu.make_async_remote_copy(
            src_ref=src, dst_ref=dst, send_sem=ssem, recv_sem=rsem, device_id=device(*to), device_id_type=MESH
        )

    def piece(k, q):
        dy, dx = OFF[k]
        n = 512 // NQ[k]
        at = pl.ds(q * n, n)
        cols = pl.ds(pl.multiple_of(rad * 256, 256), 256)
        i = BASE[k] + q
        return send(proj_v.at[k, at, :], recv_v.at[at, cols], ps_sem.at[i], pr_sem.at[i], (x + 2 * dx, y + dy, z, c))

    for k in range(8):
        inters[k].wait()
        at = pl.ds(pl.multiple_of(chunk_of(k) * 512, 512), 512)
        which = bins_v[at][None, :]
        hot = ((lax.broadcasted_iota(jnp.int32, (128, 512), 0) & 63) == which).astype(F32).astype(BF)
        lifted = lax.dot_general(hot, phl_v[...], (((0,), (0,)), ((), ())), preferred_element_type=F32)
        proj_v[k] = (interp_v[k].astype(F32) * lifted).astype(BF)
        if k == 0:
            pl.semaphore_wait(barrier, len(partners))
        if k < 7:
            for q in range(FIRST[k]):
                piece(k, q).start()
        else:
            recv_v[:, pl.ds(pl.multiple_of(rad * 256, 256), 256)] = proj_v[k]

    for k in range(8):
        coefs[k].wait()
        got = lax.dot_general(proj_v[k], coeffs_v[k], (((0,), (0,)), ((), ())), preferred_element_type=F32)
        if k == 0:
            acc_v[...] = got
        else:
            acc_v[...] += got
    part_v[...] = acc_v[...].astype(BF)

    zc = [(dz, dc) for dz in (2, 1, 3, 0) for dc in (0, 1) if dz or dc]
    sums = []
    for i, (dz, dc) in enumerate(zc):
        to_slot = ((z + dz) % 4) * 2 + (c + dc) % 2
        src = part_v.at[pl.ds(pl.multiple_of(to_slot * 32, 32), 32), :]
        sums.append(send(src, rs_v.at[i], rss_sem.at[i], rsr_sem.at[i], (x, y, z + dz, c + dc)))
        sums[-1].start()
    a = lax.broadcasted_iota(jnp.int32, (480, 512), 0)
    b = lax.broadcasted_iota(jnp.int32, (480, 512), 1)
    low = b & 63
    perm_v[...] = jnp.where(low < 60, (a == (b >> 6) * 60 + low).astype(F32), 0.0).astype(BF)
    total = part_v[pl.ds(rows, 32), :].astype(F32)
    for i in range(7):
        sums[i].wait_recv()
        total = total + rs_v[i].astype(F32)
    xs_v[...] = total.astype(BF)
    pair = send(xs_v, xr_v, xx_sem.at[0], xx_sem.at[1], (x + 1 - 2 * xl, y, z, c))
    pair.start()
    for k, q in SECOND:
        piece(k, q).start()
    table.wait()
    pair.wait_recv()
    nodes = (xs_v[...].astype(F32) + xr_v[...].astype(F32)).astype(BF)
    turned = jnp.dot(nodes, table_v[...], preferred_element_type=F32).astype(BF)
    ang_v[y, xh, pl.ds(rows, 32), :] = jnp.dot(turned, perm_v[...], preferred_element_type=F32).astype(BF)

    own = ang_v.at[y, xh, pl.ds(rows, 32), :]
    plane = []
    for i, (flip, dy) in enumerate([(0, 2), (0, 1), (0, 3), (1, 2), (1, 1), (1, 3), (1, 0)]):
        to = (3 - x if flip else x, y + dy, z, c)
        plane.append(send(own, own, pls_sem.at[i], plr_sem.at[i], to))
        plane[-1].start()
    for k, q in THIRD:
        piece(k, q).start()

    def group(g, dz):
        at = pl.multiple_of((((z + dz) % 4) * 2 + c) * 32, 32)
        return ang_v.at[:, (xh + g) % 2, pl.ds(at, 32), :]

    def other_core(g, dz):
        i = g * 4 + dz
        return send(group(g, dz), group(g, dz), cs_sem.at[i], cr_sem.at[i], (x, y, z, c + 1))

    def along(g, dz, step):
        i = g * 3 + (0 if step > 0 else 1) if dz == 0 else g * 3 + 2
        return send(group(g, dz), group(g, dz), zs_sem.at[i], zr_sem.at[i], (x, y, z + step, c))

    ups = {}
    for g in range(2):
        for i in ((0, 1, 2) if g == 0 else (3, 4, 5, 6)):
            plane[i].wait_recv()
        for step in (1, -1):
            ups[g, step] = along(g, 0, step)
            ups[g, step].start()
        ups[g, 0] = other_core(g, 0)
        ups[g, 0].start()
    for g in range(2):
        far = -1 if g == 0 else 1
        ups[g, far].wait_recv()
        back = 1 if g == 0 else -1
        relay = along(g, back, far)
        relay.start()
        ups[g, 2] = relay
        ups[g, 3] = other_core(g, back % 4)
        ups[g, 3].start()
    for g in range(2):
        far = 1 if g == 0 else -1
        ups[g, far].wait_recv()
        ups[g, 4] = other_core(g, (-far) % 4)
        ups[g, 4].start()
    for g in range(2):
        ups[g, 2].wait_recv()
        ups[g, 5] = other_core(g, 2)
        ups[g, 5].start()
    for g in range(2):
        for i in (0, 3, 4, 5):
            ups[g, i].wait_recv()

    for k in range(7):
        for q in range(NQ[k]):
            piece(k, q).wait_recv()
    lane = lax.broadcasted_iota(jnp.int32, (256, 128), 1)
    sent = {}
    for half in range(2):
        cols = ang_v[:, :, :, 256 * half : 256 * half + 256].reshape(2048, 256)
        res = jnp.dot(recv_v[...], cols, preferred_element_type=F32)
        for t in range(2):
            top, bottom = res[:256, 128 * t : 128 * t + 128], res[256:, 128 * t : 128 * t + 128]
            d = 4 * half + 2 * t
            fsend_v[d] = jnp.where(lane < 64, top, pltpu.roll(bottom, 64, 1)).astype(BF)
            fsend_v[d + 1] = jnp.where(lane < 64, pltpu.roll(top, 64, 1), bottom).astype(BF)
    for k in range(7):
        dy, dx = OFF[k]
        sent[k] = send(fsend_v.at[chunk_of(k)], frecv_v.at[k], fs_sem.at[k], fr_sem.at[k], (x + 2 * dx, y + dy, z, c))
        sent[k].start()
    outs = []
    for k in (7, 6, 5, 3, 4, 2, 1, 0):
        dy, dx = OFF[k]
        if k < 7:
            sent[k].wait_recv()
            block = frecv_v[k]
        else:
            block = fsend_v[rad]
        source = ((y - dy) % 4) * 2 + (xh + dx) % 2
        at = pl.multiple_of(source * 512, 512)
        wide = block.astype(F32)
        out_v[pl.ds(at, 256), :] = block[:, :60]
        out_v[pl.ds(at + 256, 256), :] = pltpu.roll(wide, 64, 1).astype(BF)[:, :60]
        outs.append(pltpu.make_async_copy(out_v.at[pl.ds(at, 512), :], out.at[pl.ds(at, 512), :], out_sem.at[k]))
        outs[-1].start()

    for k in range(7):
        for q in range(NQ[k]):
            piece(k, q).wait_send()
        sums[k].wait_send()
        plane[k].wait_send()
        sent[k].wait_send()
    pair.wait_send()
    for copy in ups.values():
        copy.wait_send()
    for copy in outs:
        copy.wait()


def body(coeffs, interp, phases, tables, bins):
    dma = pltpu.SemaphoreType.DMA
    return pl.pallas_call(
        kernel,
        name="coupling",
        out_shape=jax.ShapeDtypeStruct((4096, 60), BF),
        in_specs=[pl.BlockSpec(memory_space=pl.ANY)] * 5,
        out_specs=pl.BlockSpec(memory_space=pl.ANY),
        scratch_shapes=[
            pltpu.VMEM((8, 512, 256), BF),
            pltpu.VMEM((8, 512, 480), BF),
            pltpu.VMEM((64, 256), F32),
            pltpu.VMEM((4096,), jnp.int32),
            pltpu.VMEM((480, 480), BF),
            pltpu.VMEM((128, 256), BF),
            pltpu.VMEM((480, 512), BF),
            pltpu.VMEM((8, 512, 256), BF),
            pltpu.VMEM((512, 2048), BF),
            pltpu.VMEM((256, 480), F32),
            pltpu.VMEM((256, 480), BF),
            pltpu.VMEM((7, 32, 480), BF),
            pltpu.VMEM((32, 480), BF),
            pltpu.VMEM((32, 480), BF),
            pltpu.VMEM((4, 2, 256, 512), BF),
            pltpu.VMEM((8, 256, 128), BF),
            pltpu.VMEM((7, 256, 128), BF),
            pltpu.VMEM((4096, 60), BF),
            dma((8,)), dma((8,)), dma((3,)), dma((NPIECE,)), dma((NPIECE,)), dma((7,)), dma((7,)), dma((2,)),
            dma((7,)), dma((7,)), dma((6,)), dma((6,)), dma((8,)), dma((8,)), dma((7,)), dma((7,)), dma((8,)),
        ],
        compiler_params=pltpu.CompilerParams(
            collective_id=0, has_side_effects=True, vmem_limit_bytes=60 * 1024 * 1024
        ),
    )(coeffs, interp, phases, tables, bins)


def solution(mesh):
    return jax.shard_map(
        body,
        mesh=mesh,
        in_specs=(P("sph", None), P("sph", "rad"), P(None, "rad"), P("rad", None, None), P("sph")),
        out_specs=P("sph", "rad"),
        check_vma=False,
    )
```

time: 117 us -> 69.7 us (0.60); the launches traced: 115 us -> 69.4 us
  Pallas kernels: 0 us -> 60.5 us
  blocking collectives: 53.5 us -> 0 us
  waiting for transfers between devices: 33.7 us -> 0 us
  starting transfers between devices: 14.1 us -> 0 us
  matrix products: 8.47 us -> 0 us
  local copies, waits for them, and re-layouts: 5.19 us -> 8.86 us
    pallas_call x0 -> x1, Pallas kernels: none -> 60.5 us  [body(): pl.pallas_call(kernel, name='coupling', out_shape=jax.ShapeDtypeStruct((4...]
    all_to_all x3 -> x0, blocking collectives: 53.5 us -> none  [the longest x2 40.7 us: from_everyone(): return lax.all_to_all(copies, axis, split_axis=0, concat_axis=0, tiled=True)]
    all_to_all x2 -> x0, waiting for transfers between devices: 33.7 us -> none  [the longest x1 26.5 us: body(): lax.all_to_all(proj, 'rad', split_axis=0, concat_axis=1, tiled=True)]
    all_to_all x2 -> x0, starting transfers between devices: 14.1 us -> none  [the longest x1 7.74 us: summed_on_arrival(): lax.all_to_all(pieces, axis, split_axis=0, concat_axis=0, tiled=True)]
    dot_general x4 -> x0, matrix products: 8.47 us -> none  [the longest x1 3.5 us: body(): lifted = jnp.dot(onehot, phases, preferred_element_type=jnp.float32)]
    unnamed x6 -> x1, local copies, waits for them, and re-layouts: 1.01 us -> 6.44 us
    pallas_call x0 -> x1, local copies, waits for them, and re-layouts: none -> 2.42 us  [body(): pl.pallas_call(kernel, name='coupling', out_shape=jax.ShapeDtypeStruct((4...]
    all_to_all x2 -> x0, local copies, waits for them, and re-layouts: 1.39 us -> none  [body(): lax.all_to_all(own_fields, 'rad', split_axis=1, concat_axis=0, tiled=True)]
  transfers between devices with their start and end apart: 2 -> 0, of which waited for: 2 -> 0; matrix products, arithmetic and copies ran while one was open for 1% -> 0% of each run, Pallas kernels for 0% -> 0%
where the time goes in v1:
time: 69.7 us; the launch traced here: 69.4 us
  Pallas kernels  60.5 us (87%)
  local copies, waits for them, and re-layouts  8.86 us (13%)
    pallas_call x1, Pallas kernels, body(): pl.pallas_call(kernel, name='coupling', out_shape=jax.ShapeDtypeStruct((4...  60.5 us
    unnamed x1, local copies, waits for them, and re-layouts  6.44 us
    pallas_call x1, local copies, waits for them, and re-layouts, body(): pl.pallas_call(kernel, name='coupling', out_shape=jax.ShapeDtypeStruct((4...  2.42 us

profile of v1, /device:TPU:1, one launch (start us, length us, event | category | flops | bytes accessed | tf_op | source)
XLA Modules:
  0.0 69.4 jit_solution(17162267094573545258)
XLA Ops:
  0.0 6.4 %copy.6.coeffs = bf16[4096,480]{1,0:T(8,128)(2,1)} copy(bf16[4096,480]{0,1:T(8,128)(2,1)} %param.5) | data formatting | bytes 7864320 | tf_op args[0]
  6.4 60.5 %coupling.1 = bf16[4096,60]{1,0:T(8,128)(2,1)} custom-call(bf16[4096,480]{1,0:T(8,128)(2,1)} %copy.6.coeffs, bf16[4096,256]{1,0:T(8,128)(2,1)} %interp.1, f32[64,256]{1,0:T(8,128)} %phases.1, bf16[2,480,480]{2,1,0:T(8,128)(2,1)} %tables.1, s32[4096]{0:T(1024)} %bins.1), custom_call_target="tpu_custom_call" | custom-call | tf_op jit(solution)/shard_map/coupling/pallas_call | solution.py:241
  67.0 2.4 %copy.7 = bf16[4096,60]{0,1:T(8,128)(2,1)} copy(bf16[4096,60]{1,0:T(8,128)(2,1)} %coupling.1) | data formatting | bytes 983040 | tf_op jit(solution)/shard_map/coupling/pallas_call | solution.py:241

commit v2 on v1

v2 whole, which is shorter than its diff:
```python
import functools

import jax
import jax.numpy as jnp
from jax import lax
from jax.experimental import pallas as pl
from jax.experimental.pallas import tpu as pltpu
from jax.sharding import PartitionSpec as P

MESH = pl.DeviceIdType.MESH
BF = jnp.bfloat16
F32 = jnp.float32

OFF = [(2, 1), (2, 0), (1, 1), (1, 0), (3, 1), (3, 0), (0, 1), (0, 0)]
XK = [k for k, (dy, dx) in enumerate(OFF) if dx]
NQ = [4 if dx else 2 for dy, dx in OFF[:7]]
BASE = [sum(NQ[:k]) for k in range(7)]
NPIECE = sum(NQ)
FIRST = {0: 2, 1: 1, 2: 2, 3: 1, 4: 1, 5: 1, 6: 1}
SECOND = [(4, 1), (6, 1)]
REST = [(0, 2), (2, 2), (1, 1), (4, 2), (6, 2), (3, 1), (0, 3), (2, 3), (5, 1), (4, 3), (6, 3)]
THIRD = {3: REST[:3], 7: REST[3:]}
PLANE = [(0, 0), (0, 1), (0, 3), (1, 0), (0, 2), (1, 1), (1, 3), (1, 2)]
LAG = 8


def where():
    s, r = lax.axis_index("sph"), lax.axis_index("rad")
    return (r % 2) * 2 + s // 8, r // 2, (s // 2) % 4, s % 2


def device(x, y, z, c):
    x, y, z, c = x % 4, y % 4, z % 4, c % 2
    return (x % 2) * 8 + z * 2 + c, y * 2 + x // 2


def kernel(
    coeffs, interp, phases, tables, bins, out,
    interp_v, coeffs_v, phases_v, bins_v, table_v, phl_v, perm_v, proj_v, recv_v, acc_v, part_v,
    rs_v, xs_v, xr_v, ang_v, fsend_v, frecv_v, out_v,
    in_sem, co_sem, small_sem, ps_sem, pr_sem, rss_sem, rsr_sem, xx_sem, pls_sem, plr_sem,
    zs_sem, zr_sem, cs_sem, cr_sem, fs_sem, fr_sem, out_sem,
):
    x, y, z, c = where()
    xh, xl = x // 2, x % 2
    rad, slot = y * 2 + xh, z * 2 + c
    rows = pl.multiple_of(slot * 32, 32)

    def chunk_of(k):
        dy, dx = OFF[k]
        return ((y + dy) % 4) * 2 + (xh + dx) % 2

    loads = [
        pltpu.make_async_copy(phases, phases_v, small_sem.at[0]),
        pltpu.make_async_copy(bins, bins_v, small_sem.at[1]),
    ]
    inters, coefs = [], []
    for k in range(8):
        at = pl.ds(pl.multiple_of(chunk_of(k) * 512, 512), 512)
        inters.append(pltpu.make_async_copy(interp.at[at, :], interp_v.at[k], in_sem.at[k]))
        coefs.append(pltpu.make_async_copy(coeffs.at[:, at], coeffs_v.at[:, pl.ds(512 * k, 512)], co_sem.at[k]))
    table = pltpu.make_async_copy(tables.at[slot // 4], table_v, small_sem.at[2])

    partners = [(x + 2 * dx, y + dy, z, c) for dy, dx in OFF[:7]]
    partners += [(x, y, z + dz, c + dc) for dz in range(4) for dc in range(2) if dz or dc]
    partners += [(x + 1 - 2 * xl, y, z, c)]
    partners += [(3 - x, y + dy, z, c) for dy in range(4)]
    barrier = pltpu.get_barrier_semaphore()
    for partner in partners:
        pl.semaphore_signal(barrier, inc=1, device_id=device(*partner), device_id_type=MESH)
    for load in [*loads, *inters, *coefs[:2]]:
        load.start()

    for load in loads:
        load.wait()
    ph = phases_v[...]
    hi = ph.astype(BF)
    phl_v[0:64, :] = hi
    phl_v[64:128, :] = (ph - hi.astype(F32)).astype(BF)

    def send(src, dst, ssem, rsem, to):
        return pltpu.make_async_remote_copy(
            src_ref=src, dst_ref=dst, send_sem=ssem, recv_sem=rsem, device_id=device(*to), device_id_type=MESH
        )

    def piece(k, q):
        dy, dx = OFF[k]
        n = 512 // NQ[k]
        at = pl.ds(q * n, n)
        cols = pl.ds(pl.multiple_of(rad * 256, 256), 256)
        i = BASE[k] + q
        return send(proj_v.at[pl.ds(512 * k + q * n, n), :], recv_v.at[at, cols], ps_sem.at[i], pr_sem.at[i], (x + 2 * dx, y + dy, z, c))

    for k in range(8):
        inters[k].wait()
        if k < 6:
            coefs[k + 2].start()
        elif k == 6:
            table.start()
        at = pl.ds(pl.multiple_of(chunk_of(k) * 512, 512), 512)
        which = bins_v[at][None, :]
        hot = ((lax.broadcasted_iota(jnp.int32, (128, 512), 0) & 63) == which).astype(F32).astype(BF)
        lifted = lax.dot_general(hot, phl_v[...], (((0,), (0,)), ((), ())), preferred_element_type=F32)
        proj_v[512 * k : 512 * k + 512, :] = (interp_v[k].astype(F32) * lifted).astype(BF)
        if k == 0:
            pl.semaphore_wait(barrier, len(partners))
        if k < 7:
            for q in range(FIRST[k]):
                piece(k, q).start()
        else:
            recv_v[:, pl.ds(pl.multiple_of(rad * 256, 256), 256)] = proj_v[3584:4096, :]

    for h in range(2):
        for k in range(4 * h, 4 * h + 4):
            coefs[k].wait()
        at = slice(2048 * h, 2048 * h + 2048)
        got = jnp.dot(coeffs_v[:, at], proj_v[at, :], preferred_element_type=F32)
        if h == 0:
            acc_v[...] = got
        else:
            part_v[...] = (acc_v[...] + got).astype(BF).T
    zc = [(dz, dc) for dz in (2, 1, 3, 0) for dc in (0, 1) if dz or dc]
    sums = []
    for i, (dz, dc) in enumerate(zc):
        to_slot = ((z + dz) % 4) * 2 + (c + dc) % 2
        src = part_v.at[pl.ds(pl.multiple_of(to_slot * 32, 32), 32), :]
        sums.append(send(src, rs_v.at[i], rss_sem.at[i], rsr_sem.at[i], (x, y, z + dz, c + dc)))
        sums[-1].start()
    a = lax.broadcasted_iota(jnp.int32, (480, 512), 0)
    b = lax.broadcasted_iota(jnp.int32, (480, 512), 1)
    low = b & 63
    perm_v[...] = jnp.where(low < 60, (a == (b >> 6) * 60 + low).astype(F32), 0.0).astype(BF)
    total = part_v[pl.ds(rows, 32), :].astype(F32)
    for i in range(7):
        sums[i].wait_recv()
        total = total + rs_v[i].astype(F32)
    xs_v[...] = total.astype(BF)
    pair = send(xs_v, xr_v, xx_sem.at[0], xx_sem.at[1], (x + 1 - 2 * xl, y, z, c))
    pair.start()
    for k, q in SECOND:
        piece(k, q).start()
    table.wait()
    pair.wait_recv()
    nodes = (xs_v[...].astype(F32) + xr_v[...].astype(F32)).astype(BF)
    turned = jnp.dot(nodes, table_v[...], preferred_element_type=F32).astype(BF)
    ang_v[y, xh, pl.ds(rows, 32), :] = jnp.dot(turned, perm_v[...], preferred_element_type=F32).astype(BF)

    def rows_of(i, dz):
        flip, dy = PLANE[i]
        at = pl.multiple_of((((z + dz) % 4) * 2 + c) * 32, 32)
        return ang_v.at[(y - dy) % 4, (xh + flip) % 2, pl.ds(at, 32), :]

    started = []

    def go(copy):
        copy.start()
        started.append(copy)

    def across(i):
        flip, dy = PLANE[i]
        to = (3 - x if flip else x, y + dy, z, c)
        return send(rows_of(0, 0), rows_of(0, 0), pls_sem.at[i], plr_sem.at[i], to)

    def along(i, step):
        n = 3 * i + (0 if step > 0 else 1)
        return send(rows_of(i, 0), rows_of(i, 0), zs_sem.at[n], zr_sem.at[n], (x, y, z + step, c))

    def relay(i):
        step = 1 if i % 2 else -1
        n = 3 * i + 2
        return send(rows_of(i, -step), rows_of(i, -step), zs_sem.at[n], zr_sem.at[n], (x, y, z + step, c))

    def other_core(i, dz):
        n = 4 * i + dz % 4
        return send(rows_of(i, dz), rows_of(i, dz), cs_sem.at[n], cr_sem.at[n], (x, y, z, c + 1))

    def near(i):
        step = 1 if i % 2 else -1
        along(i, step).wait_recv()
        go(relay(i))
        go(other_core(i, -step))
        along(i, -step).wait_recv()
        go(other_core(i, step))

    for i in (7, 4, 5, 6, 1, 2, 3):
        go(across(i))
    for i in range(8):
        if i:
            across(i).wait_recv()
        go(along(i, 1))
        go(along(i, -1))
        go(other_core(i, 0))
        for k, q in THIRD.get(i, ()):
            piece(k, q).start()
        if i >= LAG:
            near(i - LAG)
    for i in range(8 - LAG, 8):
        near(i)
    for i in range(8):
        relay(i).wait_recv()
        go(other_core(i, 2))
    for i in range(8):
        for dz in range(4):
            other_core(i, dz).wait_recv()

    for k in range(7):
        for q in range(NQ[k]):
            piece(k, q).wait_recv()
    sent = {}
    for b in range(2):
        dys = ((2, 1), (3, 0))[b]
        cols = [ang_v[:, :, :, pl.ds(pl.multiple_of(((y + dy) % 4) * 128, 128), 128)].reshape(2048, 128) for dy in dys]
        res = jnp.dot(recv_v[...], jnp.concatenate(cols, axis=1), preferred_element_type=F32)
        fsend_v[4 * b : 4 * b + 4] = res.astype(BF).T.reshape(4, 64, 512)
        for k in range(4 * b, min(4 * b + 4, 7)):
            dy, dx = OFF[k]
            src = fsend_v.at[k // 2 * 2 + (xh + dx) % 2]
            sent[k] = send(src, frecv_v.at[k], fs_sem.at[k], fr_sem.at[k], (x + 2 * dx, y + dy, z, c))
            sent[k].start()
    outs = []
    for k in (7, 6, 5, 3, 4, 2, 1, 0):
        dy, dx = OFF[k]
        if k < 7:
            sent[k].wait_recv()
            block = frecv_v[k]
        else:
            block = fsend_v[6 + xh]
        source = ((y - dy) % 4) * 2 + (xh + dx) % 2
        at = pl.multiple_of(source * 512, 512)
        out[:, pl.ds(at, 512)] = block[:60, :]

    for k in range(7):
        for q in range(NQ[k]):
            piece(k, q).wait_send()
        sums[k].wait_send()
        sent[k].wait_send()
    pair.wait_send()
    for copy in started:
        copy.wait_send()


def body(coeffs, interp, phases, tables, bins):
    dma = pltpu.SemaphoreType.DMA
    return pl.pallas_call(
        kernel,
        name="coupling",
        out_shape=pltpu.VMEM((60, 4096), BF),
        in_specs=[pl.BlockSpec(memory_space=pl.ANY)] * 5,
        out_specs=pl.BlockSpec(memory_space=pltpu.VMEM),
        scratch_shapes=[
            pltpu.VMEM((8, 512, 256), BF),
            pltpu.VMEM((480, 4096), BF),
            pltpu.VMEM((64, 256), F32),
            pltpu.VMEM((4096,), jnp.int32),
            pltpu.VMEM((480, 480), BF),
            pltpu.VMEM((128, 256), BF),
            pltpu.VMEM((480, 512), BF),
            pltpu.VMEM((4096, 256), BF),
            pltpu.VMEM((512, 2048), BF),
            pltpu.VMEM((480, 256), F32),
            pltpu.VMEM((256, 480), BF),
            pltpu.VMEM((7, 32, 480), BF),
            pltpu.VMEM((32, 480), BF),
            pltpu.VMEM((32, 480), BF),
            pltpu.VMEM((4, 2, 256, 512), BF),
            pltpu.VMEM((8, 64, 512), BF),
            pltpu.VMEM((7, 64, 512), BF),
            pltpu.VMEM((60, 4096), BF),
            dma((8,)), dma((8,)), dma((3,)), dma((NPIECE,)), dma((NPIECE,)), dma((7,)), dma((7,)), dma((2,)),
            dma((8,)), dma((8,)), dma((24,)), dma((24,)), dma((32,)), dma((32,)), dma((7,)), dma((7,)), dma((8,)),
        ],
        compiler_params=pltpu.CompilerParams(
            collective_id=0, has_side_effects=True, vmem_limit_bytes=60 * 1024 * 1024
        ),
    )(coeffs.T, interp, phases, tables, bins).T


def solution(mesh):
    return jax.shard_map(
        body,
        mesh=mesh,
        in_specs=(P("sph", None), P("sph", "rad"), P(None, "rad"), P("rad", None, None), P("sph")),
        out_specs=P("sph", "rad"),
        check_vma=False,
    )
```

time: 69.7 us -> 52.8 us (0.76)
  Pallas kernels: 60.5 us -> 51.9 us
  local copies, waits for them, and re-layouts: 8.86 us -> 0.8 us
    pallas_call x1, Pallas kernels: 60.5 us -> 51.9 us  [body(): pl.pallas_call(kernel, name='coupling', out_shape=pltpu.VMEM((60, 4096),...]
    unnamed x1, local copies, waits for them, and re-layouts: 6.44 us -> 0.8 us
    pallas_call x1 -> x0, local copies, waits for them, and re-layouts: 2.42 us -> none  [body(): pl.pallas_call(kernel, name='coupling', out_shape=jax.ShapeDtypeStruct((4...]
where the time goes in v2:
time: 52.8 us; the launch traced here: 52.7 us
  Pallas kernels  51.9 us (98%)
  local copies, waits for them, and re-layouts  0.8 us (2%)
    pallas_call x1, Pallas kernels, body(): pl.pallas_call(kernel, name='coupling', out_shape=pltpu.VMEM((60, 4096),...  51.9 us

profile of v2, /device:TPU:1, one launch (start us, length us, event | category | flops | bytes accessed | tf_op | source)
XLA Modules:
  0.0 52.7 jit_solution(2921755632973643425)
XLA Ops:
  0.0 51.9 %coupling.1 = bf16[60,4096]{1,0:T(8,128)(2,1)S(1)} custom-call(bf16[480,4096]{1,0:T(8,128)(2,1)} %bitcast.3, bf16[4096,256]{1,0:T(8,128)(2,1)} %interp.1, f32[64,256]{1,0:T(8,128)} %phases.1, bf16[2,480,480]{2,1,0:T(8,128)(2,1)} %tables.1, s32[4096]{0:T(1024)} %bins.1), custom_call_target="tpu_custom_call" | custom-call | tf_op jit(solution)/shard_map/coupling/pallas_call | solution.py:244
  51.9 0.8 %copy.7 = bf16[4096,60]{0,1:T(8,128)(2,1)} copy(bf16[4096,60]{0,1:T(8,128)(2,1)S(1)} %bitcast.2) | data formatting | bytes 983040

commit v3 on v2

--- a/solution.py
+++ b/solution.py
@@ -17,11 +17,12 @@
 BASE = [sum(NQ[:k]) for k in range(7)]
 NPIECE = sum(NQ)
 FIRST = {0: 2, 1: 1, 2: 2, 3: 1, 4: 1, 5: 1, 6: 1}
-SECOND = [(4, 1), (6, 1)]
-REST = [(0, 2), (2, 2), (1, 1), (4, 2), (6, 2), (3, 1), (0, 3), (2, 3), (5, 1), (4, 3), (6, 3)]
+SECOND = [(6, 1)]
+REST = [(4, 1), (0, 2), (2, 2), (1, 1), (4, 2), (6, 2), (3, 1), (0, 3), (2, 3), (5, 1), (4, 3), (6, 3)]
 THIRD = {3: REST[:3], 7: REST[3:]}
 PLANE = [(0, 0), (0, 1), (0, 3), (1, 0), (0, 2), (1, 1), (1, 3), (1, 2)]
 LAG = 8
+GROUP = 4
 
 
 def where():
@@ -37,9 +38,9 @@
 def kernel(
     coeffs, interp, phases, tables, bins, out,
     interp_v, coeffs_v, phases_v, bins_v, table_v, phl_v, perm_v, proj_v, recv_v, acc_v, part_v,
-    rs_v, xs_v, xr_v, ang_v, fsend_v, frecv_v, out_v,
+    rs_v, xs_v, xr_v, ang_v, fsend_v, frecv_v,
     in_sem, co_sem, small_sem, ps_sem, pr_sem, rss_sem, rsr_sem, xx_sem, pls_sem, plr_sem,
-    zs_sem, zr_sem, cs_sem, cr_sem, fs_sem, fr_sem, out_sem,
+    zs_sem, zr_sem, cs_sem, cr_sem, fs_sem, fr_sem,
 ):
     x, y, z, c = where()
     xh, xl = x // 2, x % 2
@@ -68,9 +69,11 @@
     barrier = pltpu.get_barrier_semaphore()
     for partner in partners:
         pl.semaphore_signal(barrier, inc=1, device_id=device(*partner), device_id_type=MESH)
-    for load in [*loads, *inters, *coefs[:2]]:
+    for load in loads:
         load.start()
 
+    for load in [*inters, *coefs[:2]]:
+        load.start()
     for load in loads:
         load.wait()
     ph = phases_v[...]
@@ -91,34 +94,30 @@
         i = BASE[k] + q
         return send(proj_v.at[pl.ds(512 * k + q * n, n), :], recv_v.at[at, cols], ps_sem.at[i], pr_sem.at[i], (x + 2 * dx, y + dy, z, c))
 
+    for k0 in range(0, 8, GROUP):
+        ks = range(k0, k0 + GROUP)
+        for k in ks:
+            inters[k].wait()
+        for k in ks:
+            at = pl.ds(pl.multiple_of(chunk_of(k) * 512, 512), 512)
+            which = bins_v[at][None, :]
+            hot = ((lax.broadcasted_iota(jnp.int32, (128, 512), 0) & 63) == which).astype(F32).astype(BF)
+            lifted = lax.dot_general(hot, phl_v[...], (((0,), (0,)), ((), ())), preferred_element_type=F32)
+            proj_v[512 * k : 512 * k + 512, :] = (interp_v[k].astype(F32) * lifted).astype(BF)
+        if k0 == 0:
+            for k in range(2, 8):
+                coefs[k].start()
+            table.start()
+            pl.semaphore_wait(barrier, len(partners))
+        for k in ks:
+            if k < 7:
+                for q in range(FIRST[k]):
+                    piece(k, q).start()
+    recv_v[:, pl.ds(pl.multiple_of(rad * 256, 256), 256)] = proj_v[3584:4096, :]
+
     for k in range(8):
-        inters[k].wait()
-        if k < 6:
-            coefs[k + 2].start()
-        elif k == 6:
-            table.start()
-        at = pl.ds(pl.multiple_of(chunk_of(k) * 512, 512), 512)
-        which = bins_v[at][None, :]
-        hot = ((lax.broadcasted_iota(jnp.int32, (128, 512), 0) & 63) == which).astype(F32).astype(BF)
-        lifted = lax.dot_general(hot, phl_v[...], (((0,), (0,)), ((), ())), preferred_element_type=F32)
-        proj_v[512 * k : 512 * k + 512, :] = (interp_v[k].astype(F32) * lifted).astype(BF)
-        if k == 0:
-            pl.semaphore_wait(barrier, len(partners))
-        if k < 7:
-            for q in range(FIRST[k]):
-                piece(k, q).start()
-        else:
-            recv_v[:, pl.ds(pl.multiple_of(rad * 256, 256), 256)] = proj_v[3584:4096, :]
-
-    for h in range(2):
-        for k in range(4 * h, 4 * h + 4):
-            coefs[k].wait()
-        at = slice(2048 * h, 2048 * h + 2048)
-        got = jnp.dot(coeffs_v[:, at], proj_v[at, :], preferred_element_type=F32)
-        if h == 0:
-            acc_v[...] = got
-        else:
-            part_v[...] = (acc_v[...] + got).astype(BF).T
+        coefs[k].wait()
+    part_v[...] = lax.dot_general(proj_v[...], coeffs_v[...], (((0,), (1,)), ((), ())), preferred_element_type=F32).astype(BF)
     zc = [(dz, dc) for dz in (2, 1, 3, 0) for dc in (0, 1) if dz or dc]
     sums = []
     for i, (dz, dc) in enumerate(zc):
@@ -203,37 +202,41 @@
         for dz in range(4):
             other_core(i, dz).wait_recv()
 
-    for k in range(7):
-        for q in range(NQ[k]):
-            piece(k, q).wait_recv()
-    sent = {}
-    for b in range(2):
-        dys = ((2, 1), (3, 0))[b]
-        cols = [ang_v[:, :, :, pl.ds(pl.multiple_of(((y + dy) % 4) * 128, 128), 128)].reshape(2048, 128) for dy in dys]
-        res = jnp.dot(recv_v[...], jnp.concatenate(cols, axis=1), preferred_element_type=F32)
-        fsend_v[4 * b : 4 * b + 4] = res.astype(BF).T.reshape(4, 64, 512)
-        for k in range(4 * b, min(4 * b + 4, 7)):
+    def back(k, h):
+        dy, dx = OFF[k]
+        half = slice(256 * h, 256 * h + 256)
+        src = fsend_v.at[k // 2 * 2 + (xh + dx) % 2, :, half]
+        to = (x + 2 * dx, y + dy, z, c)
+        return send(src, frecv_v.at[k, :, half], fs_sem.at[2 * k + h], fr_sem.at[2 * k + h], to)
+
+    for h in range(2):
+        for k in range(7):
+            for q in range(NQ[k] // 2 * h, NQ[k] // 2 * (h + 1)):
+                piece(k, q).wait_recv()
+        cols = [ang_v[:, :, :, pl.ds(pl.multiple_of(((y + dy) % 4) * 128, 128), 128)] for dy in (2, 1, 3, 0)]
+        cols = jnp.concatenate([part.reshape(2048, 128) for part in cols], axis=1)
+        res = jnp.dot(recv_v[256 * h : 256 * h + 256, :], cols, preferred_element_type=F32)
+        fsend_v[:, :, 256 * h : 256 * h + 256] = res.astype(BF).T.reshape(8, 64, 256)
+        for k in range(7):
+            back(k, h).start()
+    for h in range(2):
+        for k in (7, 6, 5, 3, 4, 2, 1, 0):
             dy, dx = OFF[k]
-            src = fsend_v.at[k // 2 * 2 + (xh + dx) % 2]
-            sent[k] = send(src, frecv_v.at[k], fs_sem.at[k], fr_sem.at[k], (x + 2 * dx, y + dy, z, c))
-            sent[k].start()
-    outs = []
-    for k in (7, 6, 5, 3, 4, 2, 1, 0):
-        dy, dx = OFF[k]
-        if k < 7:
-            sent[k].wait_recv()
-            block = frecv_v[k]
-        else:
-            block = fsend_v[6 + xh]
-        source = ((y - dy) % 4) * 2 + (xh + dx) % 2
-        at = pl.multiple_of(source * 512, 512)
-        out[:, pl.ds(at, 512)] = block[:60, :]
+            half = slice(256 * h, 256 * h + 256)
+            if k < 7:
+                back(k, h).wait_recv()
+                block = frecv_v[k, :, half]
+            else:
+                block = fsend_v[6 + xh, :, half]
+            source = ((y - dy) % 4) * 2 + (xh + dx) % 2
+            out[:, pl.ds(pl.multiple_of(source * 512 + 256 * h, 256), 256)] = block[:60, :]
 
     for k in range(7):
         for q in range(NQ[k]):
             piece(k, q).wait_send()
         sums[k].wait_send()
-        sent[k].wait_send()
+        back(k, 0).wait_send()
+        back(k, 1).wait_send()
     pair.wait_send()
     for copy in started:
         copy.wait_send()
@@ -265,9 +268,8 @@
             pltpu.VMEM((4, 2, 256, 512), BF),
             pltpu.VMEM((8, 64, 512), BF),
             pltpu.VMEM((7, 64, 512), BF),
-            pltpu.VMEM((60, 4096), BF),
             dma((8,)), dma((8,)), dma((3,)), dma((NPIECE,)), dma((NPIECE,)), dma((7,)), dma((7,)), dma((2,)),
-            dma((8,)), dma((8,)), dma((24,)), dma((24,)), dma((32,)), dma((32,)), dma((7,)), dma((7,)), dma((8,)),
+            dma((8,)), dma((8,)), dma((24,)), dma((24,)), dma((32,)), dma((32,)), dma((14,)), dma((14,)),
         ],
         compiler_params=pltpu.CompilerParams(
             collective_id=0, has_side_effects=True, vmem_limit_bytes=60 * 1024 * 1024

time: 52.8 us -> 48.2 us (0.913)
  Pallas kernels: 51.9 us -> 47.3 us
    pallas_call x1, Pallas kernels: 51.9 us -> 47.3 us  [body(): pl.pallas_call(kernel, name='coupling', out_shape=pltpu.VMEM((60, 4096),...]
where the time goes in v3:
time: 48.2 us; the launch traced here: 48.1 us
  Pallas kernels  47.3 us (98%)
  local copies, waits for them, and re-layouts  0.8 us (2%)
    pallas_call x1, Pallas kernels, body(): pl.pallas_call(kernel, name='coupling', out_shape=pltpu.VMEM((60, 4096),...  47.3 us

profile of v3, /device:TPU:1, one launch (start us, length us, event | category | flops | bytes accessed | tf_op | source)
XLA Modules:
  0.0 48.1 jit_solution(14486038923596146783)
XLA Ops:
  0.0 47.3 %coupling.1 = bf16[60,4096]{1,0:T(8,128)(2,1)S(1)} custom-call(bf16[480,4096]{1,0:T(8,128)(2,1)} %bitcast.3, bf16[4096,256]{1,0:T(8,128)(2,1)} %interp.1, f32[64,256]{1,0:T(8,128)} %phases.1, bf16[2,480,480]{2,1,0:T(8,128)(2,1)} %tables.1, s32[4096]{0:T(1024)} %bins.1), custom_call_target="tpu_custom_call" | custom-call | tf_op jit(solution)/shard_map/coupling/pallas_call | solution.py:247
  47.3 0.8 %copy.7 = bf16[4096,60]{0,1:T(8,128)(2,1)} copy(bf16[4096,60]{0,1:T(8,128)(2,1)S(1)} %bitcast.2) | data formatting | bytes 983040

commit v4 on v3

--- a/solution.py
+++ b/solution.py
@@ -18,10 +18,12 @@
 NPIECE = sum(NQ)
 FIRST = {0: 2, 1: 1, 2: 2, 3: 1, 4: 1, 5: 1, 6: 1}
 SECOND = [(6, 1)]
-REST = [(4, 1), (0, 2), (2, 2), (1, 1), (4, 2), (6, 2), (3, 1), (0, 3), (2, 3), (5, 1), (4, 3), (6, 3)]
+REST = [(4, 1), (0, 2), (2, 2), (1, 1), (4, 2), (6, 2), (0, 3), (2, 3), (4, 3), (6, 3)]
 THIRD = {3: REST[:3], 7: REST[3:]}
 PLANE = [(0, 0), (0, 1), (0, 3), (1, 0), (0, 2), (1, 1), (1, 3), (1, 2)]
 LAG = 8
+EARLY = [(3, 1), (5, 1)]
+EXTRA = []
 GROUP = 4
 
 
@@ -40,7 +42,7 @@
     interp_v, coeffs_v, phases_v, bins_v, table_v, phl_v, perm_v, proj_v, recv_v, acc_v, part_v,
     rs_v, xs_v, xr_v, ang_v, fsend_v, frecv_v,
     in_sem, co_sem, small_sem, ps_sem, pr_sem, rss_sem, rsr_sem, xx_sem, pls_sem, plr_sem,
-    zs_sem, zr_sem, cs_sem, cr_sem, fs_sem, fr_sem,
+    zs_sem, zr_sem, cs_sem, cr_sem, fs_sem, fr_sem, later,
 ):
     x, y, z, c = where()
     xh, xl = x // 2, x % 2
@@ -63,12 +65,18 @@
     table = pltpu.make_async_copy(tables.at[slot // 4], table_v, small_sem.at[2])
 
     partners = [(x + 2 * dx, y + dy, z, c) for dy, dx in OFF[:7]]
-    partners += [(x, y, z + dz, c + dc) for dz in range(4) for dc in range(2) if dz or dc]
-    partners += [(x + 1 - 2 * xl, y, z, c)]
+    partners += [(x, y, z, c + 1), (x + 1 - 2 * xl, y, z, c)]
     partners += [(3 - x, y + dy, z, c) for dy in range(4)]
     barrier = pltpu.get_barrier_semaphore()
     for partner in partners:
         pl.semaphore_signal(barrier, inc=1, device_id=device(*partner), device_id_type=MESH)
+    for dz in range(1, 4):
+
+        @pl.when(z + dz < 4)
+        def _():
+            for dc in range(2):
+                pl.semaphore_signal(barrier, inc=1, device_id=device(x, y, z + dz, c + dc), device_id_type=MESH)
+
     for load in loads:
         load.start()
 
@@ -108,16 +116,30 @@
             for k in range(2, 8):
                 coefs[k].start()
             table.start()
-            pl.semaphore_wait(barrier, len(partners))
+            pl.semaphore_wait(barrier, len(partners) + 2 * z)
+            for dz in range(1, 4):
+
+                @pl.when(z + dz >= 4)
+                def _():
+                    for dc in range(2):
+                        pl.semaphore_signal(later, inc=1, device_id=device(x, y, z + dz, c + dc), device_id_type=MESH)
+
         for k in ks:
             if k < 7:
                 for q in range(FIRST[k]):
                     piece(k, q).start()
+    for (k, q), last in EXTRA:
+        pl.when(z <= last)(piece(k, q).start)
     recv_v[:, pl.ds(pl.multiple_of(rad * 256, 256), 256)] = proj_v[3584:4096, :]
 
     for k in range(8):
         coefs[k].wait()
     part_v[...] = lax.dot_general(proj_v[...], coeffs_v[...], (((0,), (1,)), ((), ())), preferred_element_type=F32).astype(BF)
+
+    @pl.when(z < 3)
+    def _():
+        pl.semaphore_wait(later, 6 - 2 * z)
+
     zc = [(dz, dc) for dz in (2, 1, 3, 0) for dc in (0, 1) if dz or dc]
     sums = []
     for i, (dz, dc) in enumerate(zc):
@@ -182,13 +204,23 @@
         go(other_core(i, step))
 
     for i in (7, 4, 5, 6, 1, 2, 3):
-        go(across(i))
+        across(i).start()
+    for step in (1, -1):
+        go(along(0, step))
+    go(other_core(0, 0))
+    for i in (7, 4, 5, 6, 1, 2, 3):
+        across(i).wait_send()
+    for k, q in EARLY:
+        piece(k, q).start()
     for i in range(8):
         if i:
             across(i).wait_recv()
-        go(along(i, 1))
-        go(along(i, -1))
-        go(other_core(i, 0))
+            go(along(i, 1))
+            go(along(i, -1))
+            go(other_core(i, 0))
+        if i == 7:
+            for (k, q), last in EXTRA:
+                pl.when(z > last)(piece(k, q).start)
         for k, q in THIRD.get(i, ()):
             piece(k, q).start()
         if i >= LAG:
@@ -269,7 +301,7 @@
             pltpu.VMEM((8, 64, 512), BF),
             pltpu.VMEM((7, 64, 512), BF),
             dma((8,)), dma((8,)), dma((3,)), dma((NPIECE,)), dma((NPIECE,)), dma((7,)), dma((7,)), dma((2,)),
-            dma((8,)), dma((8,)), dma((24,)), dma((24,)), dma((32,)), dma((32,)), dma((14,)), dma((14,)),
+            dma((8,)), dma((8,)), dma((24,)), dma((24,)), dma((32,)), dma((32,)), dma((14,)), dma((14,)), pltpu.SemaphoreType.REGULAR,
         ],
         compiler_params=pltpu.CompilerParams(
             collective_id=0, has_side_effects=True, vmem_limit_bytes=60 * 1024 * 1024

time: 48.2 us -> 48 us (level)
  no operation moved by 1% of the time
where the time goes in v4:
time: 48 us; the launch traced here: 47.9 us
  Pallas kernels  47.1 us (98%)
  local copies, waits for them, and re-layouts  0.8 us (2%)
    pallas_call x1, Pallas kernels, body(): pl.pallas_call(kernel, name='coupling', out_shape=pltpu.VMEM((60, 4096),...  47.1 us

profile of v4, /device:TPU:1, one launch (start us, length us, event | category | flops | bytes accessed | tf_op | source)
XLA Modules:
  0.0 47.9 jit_solution(12016248243893120961)
XLA Ops:
  0.0 47.1 %coupling.1 = bf16[60,4096]{1,0:T(8,128)(2,1)S(1)} custom-call(bf16[480,4096]{1,0:T(8,128)(2,1)} %bitcast.3, bf16[4096,256]{1,0:T(8,128)(2,1)} %interp.1, f32[64,256]{1,0:T(8,128)} %phases.1, bf16[2,480,480]{2,1,0:T(8,128)(2,1)} %tables.1, s32[4096]{0:T(1024)} %bins.1), custom_call_target="tpu_custom_call" | custom-call | tf_op jit(solution)/shard_map/coupling/pallas_call | solution.py:279
  47.1 0.8 %copy.7 = bf16[4096,60]{0,1:T(8,128)(2,1)} copy(bf16[4096,60]{0,1:T(8,128)(2,1)S(1)} %bitcast.2) | data formatting | bytes 983040

commit v5 on v4

--- a/solution.py
+++ b/solution.py
@@ -18,13 +18,13 @@
 NPIECE = sum(NQ)
 FIRST = {0: 2, 1: 1, 2: 2, 3: 1, 4: 1, 5: 1, 6: 1}
 SECOND = [(6, 1)]
-REST = [(4, 1), (0, 2), (2, 2), (1, 1), (4, 2), (6, 2), (0, 3), (2, 3), (4, 3), (6, 3)]
-THIRD = {3: REST[:3], 7: REST[3:]}
+REST = [(4, 1), (0, 2), (2, 2), (1, 1), (4, 2), (0, 3), (2, 3), (4, 3), (6, 3)]
+THIRD = {7: REST}
 PLANE = [(0, 0), (0, 1), (0, 3), (1, 0), (0, 2), (1, 1), (1, 3), (1, 2)]
 LAG = 8
 EARLY = [(3, 1), (5, 1)]
-EXTRA = []
-GROUP = 4
+EXTRA = [((6, 2), 0)]
+GROUP = 2
 
 
 def where():
@@ -203,12 +203,12 @@
         along(i, -step).wait_recv()
         go(other_core(i, step))
 
-    for i in (7, 4, 5, 6, 1, 2, 3):
+    for i in (4, 1, 2, 5, 6, 3, 7):
         across(i).start()
     for step in (1, -1):
         go(along(0, step))
     go(other_core(0, 0))
-    for i in (7, 4, 5, 6, 1, 2, 3):
+    for i in (4, 1, 2, 5, 6, 3, 7):
         across(i).wait_send()
     for k, q in EARLY:
         piece(k, q).start()

time: 48 us -> 47.2 us (0.983)
  Pallas kernels: 47.1 us -> 46.3 us
    pallas_call x1, Pallas kernels: 47.1 us -> 46.3 us  [body(): pl.pallas_call(kernel, name='coupling', out_shape=pltpu.VMEM((60, 4096),...]
where the time goes in v5:
time: 47.2 us; the launch traced here: 47.1 us
  Pallas kernels  46.3 us (98%)
  local copies, waits for them, and re-layouts  0.8 us (2%)
    pallas_call x1, Pallas kernels, body(): pl.pallas_call(kernel, name='coupling', out_shape=pltpu.VMEM((60, 4096),...  46.3 us

profile of v5, /device:TPU:1, one launch (start us, length us, event | category | flops | bytes accessed | tf_op | source)
XLA Modules:
  0.0 47.1 jit_solution(16110178516708705253)
XLA Ops:
  0.0 46.3 %coupling.1 = bf16[60,4096]{1,0:T(8,128)(2,1)S(1)} custom-call(bf16[480,4096]{1,0:T(8,128)(2,1)} %bitcast.3, bf16[4096,256]{1,0:T(8,128)(2,1)} %interp.1, f32[64,256]{1,0:T(8,128)} %phases.1, bf16[2,480,480]{2,1,0:T(8,128)(2,1)} %tables.1, s32[4096]{0:T(1024)} %bins.1), custom_call_target="tpu_custom_call" | custom-call | tf_op jit(solution)/shard_map/coupling/pallas_call | solution.py:279
  46.3 0.8 %copy.7 = bf16[4096,60]{0,1:T(8,128)(2,1)} copy(bf16[4096,60]{0,1:T(8,128)(2,1)S(1)} %bitcast.2) | data formatting | bytes 983040

commit v6 on v5

--- a/solution.py
+++ b/solution.py
@@ -248,11 +248,13 @@
         cols = [ang_v[:, :, :, pl.ds(pl.multiple_of(((y + dy) % 4) * 128, 128), 128)] for dy in (2, 1, 3, 0)]
         cols = jnp.concatenate([part.reshape(2048, 128) for part in cols], axis=1)
         res = jnp.dot(recv_v[256 * h : 256 * h + 256, :], cols, preferred_element_type=F32)
-        fsend_v[:, :, 256 * h : 256 * h + 256] = res.astype(BF).T.reshape(8, 64, 256)
-        for k in range(7):
-            back(k, h).start()
+        for b in range(2):
+            part = res[:, 256 * b : 256 * b + 256].astype(BF).T
+            fsend_v[4 * b : 4 * b + 4, :, 256 * h : 256 * h + 256] = part.reshape(4, 64, 256)
+            for k in range(4 * b, min(4 * b + 4, 7)):
+                back(k, h).start()
     for h in range(2):
-        for k in (7, 6, 5, 3, 4, 2, 1, 0):
+        for k in (7, 5, 3, 6, 1, 4, 2, 0):
             dy, dx = OFF[k]
             half = slice(256 * h, 256 * h + 256)
             if k < 7:

time: 47.2 us -> 47.2 us (level)
  no operation moved by 1% of the time
where the time goes in v6:
time: 47.2 us; the launch traced here: 47.1 us
  Pallas kernels  46.2 us (98%)
  local copies, waits for them, and re-layouts  0.8 us (2%)
    pallas_call x1, Pallas kernels, body(): pl.pallas_call(kernel, name='coupling', out_shape=pltpu.VMEM((60, 4096),...  46.2 us

profile of v6, /device:TPU:1, one launch (start us, length us, event | category | flops | bytes accessed | tf_op | source)
XLA Modules:
  0.0 47.1 jit_solution(5130807969162982536)
XLA Ops:
  0.0 46.2 %coupling.1 = bf16[60,4096]{1,0:T(8,128)(2,1)S(1)} custom-call(bf16[480,4096]{1,0:T(8,128)(2,1)} %bitcast.3, bf16[4096,256]{1,0:T(8,128)(2,1)} %interp.1, f32[64,256]{1,0:T(8,128)} %phases.1, bf16[2,480,480]{2,1,0:T(8,128)(2,1)} %tables.1, s32[4096]{0:T(1024)} %bins.1), custom_call_target="tpu_custom_call" | custom-call | tf_op jit(solution)/shard_map/coupling/pallas_call | solution.py:281
  46.3 0.8 %copy.7 = bf16[4096,60]{0,1:T(8,128)(2,1)} copy(bf16[4096,60]{0,1:T(8,128)(2,1)S(1)} %bitcast.2) | data formatting | bytes 983040

commit v7 on v5

--- a/solution.py
+++ b/solution.py
@@ -147,13 +147,15 @@
         src = part_v.at[pl.ds(pl.multiple_of(to_slot * 32, 32), 32), :]
         sums.append(send(src, rs_v.at[i], rss_sem.at[i], rsr_sem.at[i], (x, y, z + dz, c + dc)))
         sums[-1].start()
+    total = part_v[pl.ds(rows, 32), :].astype(F32)
+    sums[0].wait_recv()
     a = lax.broadcasted_iota(jnp.int32, (480, 512), 0)
     b = lax.broadcasted_iota(jnp.int32, (480, 512), 1)
     low = b & 63
     perm_v[...] = jnp.where(low < 60, (a == (b >> 6) * 60 + low).astype(F32), 0.0).astype(BF)
-    total = part_v[pl.ds(rows, 32), :].astype(F32)
     for i in range(7):
-        sums[i].wait_recv()
+        if i:
+            sums[i].wait_recv()
         total = total + rs_v[i].astype(F32)
     xs_v[...] = total.astype(BF)
     pair = send(xs_v, xr_v, xx_sem.at[0], xx_sem.at[1], (x + 1 - 2 * xl, y, z, c))
@@ -252,7 +254,7 @@
         for k in range(7):
             back(k, h).start()
     for h in range(2):
-        for k in (7, 6, 5, 3, 4, 2, 1, 0):
+        for k in (7, 5, 3, 6, 1, 4, 2, 0):
             dy, dx = OFF[k]
             half = slice(256 * h, 256 * h + 256)
             if k < 7:

time: 47.2 us -> 47.2 us (level)
  no operation moved by 1% of the time
where the time goes in v7:
time: 47.2 us; the launch traced here: 47.1 us
  Pallas kernels  46.3 us (98%)
  local copies, waits for them, and re-layouts  0.8 us (2%)
    pallas_call x1, Pallas kernels, body(): pl.pallas_call(kernel, name='coupling', out_shape=pltpu.VMEM((60, 4096),...  46.3 us

profile of v7, /device:TPU:1, one launch (start us, length us, event | category | flops | bytes accessed | tf_op | source)
XLA Modules:
  0.0 47.1 jit_solution(16995735014080099047)
XLA Ops:
  0.0 46.3 %coupling.1 = bf16[60,4096]{1,0:T(8,128)(2,1)S(1)} custom-call(bf16[480,4096]{1,0:T(8,128)(2,1)} %bitcast.3, bf16[4096,256]{1,0:T(8,128)(2,1)} %interp.1, f32[64,256]{1,0:T(8,128)} %phases.1, bf16[2,480,480]{2,1,0:T(8,128)(2,1)} %tables.1, s32[4096]{0:T(1024)} %bins.1), custom_call_target="tpu_custom_call" | custom-call | tf_op jit(solution)/shard_map/coupling/pallas_call | solution.py:281
  46.3 0.8 %copy.7 = bf16[4096,60]{0,1:T(8,128)(2,1)} copy(bf16[4096,60]{0,1:T(8,128)(2,1)S(1)} %bitcast.2) | data formatting | bytes 983040
